TPU v7x, 32 devices: a whole 2x2x4 slice. The times are simulated.
32 devices in a mesh: seq: 8 (over z, y), head: 4 (over x, core).
Axes of the slice: x: 2, y: 2, z: 4, core: 2. Of those that a mesh axis runs over, the one named last changes fastest.
Arguments:
- queries: bfloat16 [2048, 8192], P('seq', 'head'), may hold values from -40 to 40
- key_rows: bfloat16 [2048, 8192], P('seq', 'head'), may hold values from -20 to 20
- value_rows: bfloat16 [2048, 8192], P('seq', 'head'), may hold values from -8 to 8
Outputs:
- attended: bfloat16 [2048, 8192], P('seq', 'head')
All inputs are finite; a program needn't handle non-finite values.
Results may differ from a plain program's by a relative error of at most 0.0043.
Values may be sent and summed in bfloat16 or wider, within the bound.
A program may use at most 128 MiB of HBM per device.

v0:
```python
import functools
import math

import jax
import jax.numpy as jnp
from jax import lax
from jax.experimental import pallas as pl
from jax.experimental.pallas import tpu as pltpu
from jax.sharding import PartitionSpec as P

HEAD_DIM = 128
BLOCK = 128
POOL = 64
MID_REACH = 3
FAR_REACH = 9

HALF = BLOCK // 2
QUARTER = BLOCK // 4
GROUP_BLOCKS = 4
GROUP_ROWS = GROUP_BLOCKS * BLOCK
COARSE_SLOT = 16
COARSE_USED = GROUP_ROWS // POOL

FINE_LOW, FINE_BLOCKS = -1, GROUP_BLOCKS + 2
MID_LOW, MID_BLOCKS = -MID_REACH, GROUP_BLOCKS + 2 * MID_REACH
FAR_LOW, FAR_BLOCKS = -FAR_REACH, GROUP_BLOCKS + 2 * FAR_REACH

KIND_K, KIND_V, KIND_Q, KIND_O = 0, 1, 2, 3
FIRST_HOP = (
    (4, 1, "fine", 3, 1, -1),
    (5, -1, "fine", 0, 1, 4),
    (6, 1, "mid", 1, 2, -3),
    (7, -1, "mid", 1, 2, 5),
    (8, 1, "far", 0, 1, -4),
    (9, -1, "far", 3, 1, 7),
)
SECOND_HOP = (
    (10, 2, "far", -4, 4, -8),
    (11, -2, "far", 4, 4, 8),
)
THIRD_HOP = (
    (12, 3, "far", -5, 1, -9),
    (13, -3, "far", 8, 1, 12),
)
ROUTES = FIRST_HOP + SECOND_HOP + THIRD_HOP
RELAY_LAG, FORWARD_LAG, ATTEND_LAG = 2, 3, 4
KINDS = 14
MESH = pl.DeviceIdType.MESH


def hop_of(offset):
    return 1 if offset > 0 else -1


def pool_matrix(out_rows, in_rows, group_rows):
    row = lax.broadcasted_iota(jnp.int32, (out_rows, in_rows), 0)
    col = lax.broadcasted_iota(jnp.int32, (out_rows, in_rows), 1)
    return jnp.where(col // group_rows == row, 1.0 / group_rows, 0.0).astype(jnp.bfloat16)


def pooled(source, out_rows, group_rows):
    weights = pool_matrix(out_rows, source.shape[0], group_rows)
    return jnp.dot(weights, source, preferred_element_type=jnp.float32).astype(jnp.bfloat16)


def kernel(
    groups, q_ref, k_ref, v_ref, o_ref,
    q_rows, fine, mid, far, coarse, out_rows, bias,
    send, recv, coarse_send, coarse_recv, local,
):
    me = lax.axis_index("seq")
    group = me // 2
    parity = me % 2
    partner = me + 1 - 2 * parity
    rows_dev = q_ref.shape[0]
    chunks = q_rows.shape[0]
    half_cols = chunks * HEAD_DIM
    own_first = pl.multiple_of(parity * rows_dev, rows_dev)
    other_first = pl.multiple_of((1 - parity) * rows_dev, rows_dev)
    levels = {"fine": (fine, BLOCK, FINE_LOW), "mid": (mid, HALF, MID_LOW), "far": (far, QUARTER, FAR_LOW)}

    def own_cols(chunk):
        return pl.ds(pl.multiple_of(parity * half_cols + chunk * HEAD_DIM, HEAD_DIM), HEAD_DIM)

    def other_cols(chunk):
        return pl.ds(pl.multiple_of((1 - parity) * half_cols + chunk * HEAD_DIM, HEAD_DIM), HEAD_DIM)

    def remote(src, dst, kind, chunk, target):
        return pltpu.make_async_remote_copy(
            src_ref=src, dst_ref=dst, send_sem=send.at[chunk, kind], recv_sem=recv.at[chunk, kind],
            device_id={"seq": target}, device_id_type=MESH,
        )

    def exchange(kind, chunk):
        if kind == KIND_Q:
            return remote(
                q_ref.at[:, other_cols(chunk)], q_rows.at[chunk, pl.ds(own_first, rows_dev)],
                kind, chunk, partner,
            )
        if kind == KIND_O:
            return remote(
                out_rows.at[chunk, pl.ds(other_first, rows_dev)], o_ref.at[:, own_cols(chunk)],
                kind, chunk, partner,
            )
        source = k_ref if kind == KIND_K else v_ref
        return remote(
            source.at[:, other_cols(chunk)], fine.at[chunk, kind, pl.ds(BLOCK + own_first, rows_dev)],
            kind, chunk, partner,
        )

    def routed(route, chunk):
        kind, offset, level, first, count, landing = route
        window, unit, low = levels[level]
        return remote(
            window.at[chunk, :, pl.ds((first - low) * unit, count * unit)],
            window.at[chunk, :, pl.ds((landing - low) * unit, count * unit)],
            kind, chunk, me + 2 * hop_of(offset),
        )

    def coarse_copy(chunk, step):
        target = lax.rem(group + step, groups) * 2 + parity
        slot = pl.ds(pl.multiple_of(group * COARSE_SLOT, COARSE_SLOT), COARSE_SLOT)
        return pltpu.make_async_remote_copy(
            src_ref=coarse.at[chunk, :, slot], dst_ref=coarse.at[chunk, :, slot],
            send_sem=coarse_send.at[chunk, step], recv_sem=coarse_recv.at[chunk, step],
            device_id={"seq": target}, device_id_type=MESH,
        )

    def inside(offset):
        return (group + offset >= 0) & (group + offset < groups)

    def start_routes(routes, chunk):
        for route in routes:
            hop = hop_of(route[1])

            @pl.when(inside(hop) & inside(hop - route[1]))
            def _():
                routed(route, chunk).start()

    def await_routes(routes, chunk):
        for route in routes:
            @pl.when(inside(-route[1]))
            def _():
                routed(route, chunk).wait_recv()

    def own_copy(kind, chunk):
        if kind == KIND_Q:
            source, target = q_ref, q_rows.at[chunk, pl.ds(own_first, rows_dev)]
        else:
            source = k_ref if kind == KIND_K else v_ref
            target = fine.at[chunk, kind, pl.ds(BLOCK + own_first, rows_dev)]
        return pltpu.make_async_copy(source.at[:, own_cols(chunk)], target, local.at[chunk, kind])

    def own_result(chunk):
        return pltpu.make_async_copy(
            out_rows.at[chunk, pl.ds(own_first, rows_dev)], o_ref.at[:, own_cols(chunk)],
            local.at[chunk, KIND_O],
        )

    barrier = pltpu.get_barrier_semaphore()
    pl.semaphore_signal(barrier, inc=1, device_id={"seq": partner}, device_id_type=MESH)

    @pl.loop(1, groups)
    def _(step):
        target = lax.rem(group + step, groups) * 2 + parity
        pl.semaphore_signal(barrier, inc=1, device_id={"seq": target}, device_id_type=MESH)

    pl.semaphore_wait(barrier, groups)

    @pl.loop(0, chunks)
    def _(chunk):
        exchange(KIND_K, chunk).start()
        exchange(KIND_V, chunk).start()
        own_copy(KIND_K, chunk).start()
        own_copy(KIND_V, chunk).start()

    @pl.loop(0, chunks)
    def _(chunk):
        exchange(KIND_Q, chunk).start()
        own_copy(KIND_Q, chunk).start()

    for _, offset, level, _, count, landing in ROUTES:
        window, unit, low = levels[level]

        @pl.when(jnp.logical_not(inside(-offset)))
        def _():
            @pl.loop(0, chunks)
            def _(chunk):
                window[chunk, :, pl.ds((landing - low) * unit, count * unit)] = jnp.zeros(
                    (2, count * unit, HEAD_DIM), jnp.bfloat16
                )

    atoms = bias.shape[1]
    total_blocks = groups * GROUP_BLOCKS
    place = lax.broadcasted_iota(jnp.int32, (1, atoms), 1)
    windows_end = 8 * BLOCK
    for block in range(GROUP_BLOCKS):
        rel = jnp.where(
            place < 384,
            block - 1 + place // BLOCK,
            jnp.where(
                place < 512,
                block - 3 + (place - 384) // HALF,
                jnp.where(
                    place < 640,
                    block + 2 + (place - 512) // HALF,
                    jnp.where(
                        place < 832,
                        block - 9 + (place - 640) // QUARTER,
                        block + 4 + (place - 832) // QUARTER,
                    ),
                ),
            ),
        )
        here = group * GROUP_BLOCKS + rel
        held = (here >= 0) & (here < total_blocks)
        late = place - windows_end
        slot_row = late % COARSE_SLOT
        coarse_block = late // COARSE_SLOT * GROUP_BLOCKS + slot_row * POOL // BLOCK
        apart = jnp.abs(coarse_block - (group * GROUP_BLOCKS + block)) > FAR_REACH
        allowed = ((place < windows_end) & held) | (
            (place >= windows_end) & (slot_row < COARSE_USED) & apart
        )
        log_size = jnp.where(
            place < 384, 0.0, jnp.where(place < 640, 1.0, jnp.where(place < windows_end, 2.0, math.log2(POOL)))
        )
        bias[pl.ds(block, 1), :] = jnp.where(allowed, log_size, -jnp.inf)

    def gather(chunk):
        for kind in (KIND_K, KIND_V):
            own_copy(kind, chunk).wait()
            exchange(kind, chunk).wait_recv()
        start_routes(FIRST_HOP[:2], chunk)
        slot = pl.ds(pl.multiple_of(group * COARSE_SLOT, COARSE_SLOT), COARSE_SLOT)
        for side in range(2):
            rows = fine[chunk, side, BLOCK : BLOCK + GROUP_ROWS]
            twos = pooled(rows, GROUP_ROWS // 2, 2)
            fours = pooled(twos, GROUP_ROWS // 4, 2)
            mid[chunk, side, -MID_LOW * HALF : (GROUP_BLOCKS - MID_LOW) * HALF] = twos
            far[chunk, side, -FAR_LOW * QUARTER : (GROUP_BLOCKS - FAR_LOW) * QUARTER] = fours
            coarse[chunk, side, slot] = pooled(fours, COARSE_SLOT, POOL // 4)
        start_routes(FIRST_HOP[2:], chunk)

        @pl.loop(1, groups)
        def _(step):
            @pl.when(jnp.abs(lax.rem(group + step, groups) - group) > 2)
            def _():
                coarse_copy(chunk, step).start()

    def relay(chunk):
        await_routes(FIRST_HOP, chunk)
        for side in range(2):
            mid[chunk, side, 2 * HALF : 3 * HALF] = pooled(fine[chunk, side, :BLOCK], HALF, 2)
            mid[chunk, side, 7 * HALF : 8 * HALF] = pooled(fine[chunk, side, 5 * BLOCK :], HALF, 2)
            far[chunk, side, 6 * QUARTER : 9 * QUARTER] = pooled(
                mid[chunk, side, : 3 * HALF], 3 * QUARTER, 2
            )
            far[chunk, side, 13 * QUARTER : 16 * QUARTER] = pooled(
                mid[chunk, side, 7 * HALF :], 3 * QUARTER, 2
            )
        start_routes(SECOND_HOP, chunk)

    def forward(chunk):
        await_routes(SECOND_HOP, chunk)
        start_routes(THIRD_HOP, chunk)

    scale = math.log2(math.e) / math.sqrt(HEAD_DIM)

    def attend(chunk):
        own_copy(KIND_Q, chunk).wait()
        exchange(KIND_Q, chunk).wait_recv()
        await_routes(THIRD_HOP, chunk)

        @pl.loop(1, groups)
        def _(step):
            giver = lax.rem(group - step + groups, groups)
            origin = pl.ds(pl.multiple_of(giver * COARSE_SLOT, COARSE_SLOT), COARSE_SLOT)

            @pl.when(jnp.abs(giver - group) > 2)
            def _():
                pltpu.make_async_remote_copy(
                    src_ref=coarse.at[chunk, :, origin], dst_ref=coarse.at[chunk, :, origin],
                    send_sem=coarse_send.at[chunk, step], recv_sem=coarse_recv.at[chunk, step],
                    device_id={"seq": partner}, device_id_type=MESH,
                ).wait_recv()

        for offset in (-2, -1, 1, 2):
            @pl.when(inside(offset))
            def _():
                near = pl.ds(pl.multiple_of((group + offset) * COARSE_SLOT, COARSE_SLOT), COARSE_SLOT)
                first = (offset * GROUP_BLOCKS - FAR_LOW) * QUARTER
                for side in range(2):
                    fours = far[chunk, side, first : first + GROUP_ROWS // 4]
                    coarse[chunk, side, near] = pooled(fours, COARSE_SLOT, POOL // 4)

        for block in range(GROUP_BLOCKS):
            def atom_rows(side):
                return jnp.concatenate(
                    [
                        fine[chunk, side, block * BLOCK : (block + 3) * BLOCK],
                        mid[chunk, side, block * HALF : (block + 2) * HALF],
                        mid[chunk, side, (block + 5) * HALF : (block + 7) * HALF],
                        far[chunk, side, block * QUARTER : (block + 6) * QUARTER],
                        far[chunk, side, (block + 13) * QUARTER : (block + 19) * QUARTER],
                        coarse[chunk, side],
                    ],
                    axis=0,
                )

            scores = lax.dot_general(
                q_rows[chunk, block * BLOCK : (block + 1) * BLOCK], atom_rows(0),
                (((1,), (1,)), ((), ())), preferred_element_type=jnp.float32,
            ) * scale + bias[pl.ds(block, 1), :]
            row_top = jnp.max(scores, axis=1, keepdims=True)
            exp_terms = jnp.exp2(scores - row_top)
            denominator = jnp.sum(exp_terms, axis=1, keepdims=True)
            weighted = jnp.dot(
                exp_terms.astype(jnp.bfloat16), atom_rows(1), preferred_element_type=jnp.float32
            )
            out_rows[chunk, block * BLOCK : (block + 1) * BLOCK] = (weighted / denominator).astype(
                jnp.bfloat16
            )
        exchange(KIND_O, chunk).start()
        own_result(chunk).start()

    stages = ((gather, 0), (relay, RELAY_LAG), (forward, FORWARD_LAG), (attend, ATTEND_LAG))

    @pl.loop(0, chunks + ATTEND_LAG)
    def _(step):
        for stage, lag in stages:
            @pl.when((step >= lag) & (step < chunks + lag))
            def _():
                stage(step - lag)

    @pl.loop(0, chunks)
    def _(chunk):
        own_result(chunk).wait()
        exchange(KIND_O, chunk).wait_recv()
        for kind in (KIND_K, KIND_V, KIND_Q, KIND_O):
            exchange(kind, chunk).wait_send()
        for route in ROUTES:
            hop = hop_of(route[1])

            @pl.when(inside(hop) & inside(hop - route[1]))
            def _():
                routed(route, chunk).wait_send()

        @pl.loop(1, groups)
        def _(step):
            @pl.when(jnp.abs(lax.rem(group + step, groups) - group) > 2)
            def _():
                coarse_copy(chunk, step).wait_send()


def per_device(queries, key_rows, value_rows):
    rows_dev, cols = queries.shape
    groups = lax.axis_size("seq") // 2
    chunks = cols // 2 // HEAD_DIM
    atoms = 8 * BLOCK + groups * COARSE_SLOT
    bf16 = jnp.bfloat16
    placed = pl.BlockSpec(memory_space=pltpu.HBM)
    return pl.pallas_call(
        functools.partial(kernel, groups),
        out_shape=jax.ShapeDtypeStruct(queries.shape, bf16),
        in_specs=[placed] * 3,
        out_specs=placed,
        scratch_shapes=[
            pltpu.VMEM((chunks, 2 * rows_dev, HEAD_DIM), bf16),
            pltpu.VMEM((chunks, 2, FINE_BLOCKS * BLOCK, HEAD_DIM), bf16),
            pltpu.VMEM((chunks, 2, MID_BLOCKS * HALF, HEAD_DIM), bf16),
            pltpu.VMEM((chunks, 2, FAR_BLOCKS * QUARTER, HEAD_DIM), bf16),
            pltpu.VMEM((chunks, 2, groups * COARSE_SLOT, HEAD_DIM), bf16),
            pltpu.VMEM((chunks, 2 * rows_dev, HEAD_DIM), bf16),
            pltpu.VMEM((8, atoms), jnp.float32),
            pltpu.SemaphoreType.DMA((chunks, KINDS)),
            pltpu.SemaphoreType.DMA((chunks, KINDS)),
            pltpu.SemaphoreType.DMA((chunks, groups)),
            pltpu.SemaphoreType.DMA((chunks, groups)),
            pltpu.SemaphoreType.DMA((chunks, 4)),
        ],
        compiler_params=pltpu.CompilerParams(
            collective_id=0, has_side_effects=True, vmem_limit_bytes=48 * 1024 * 1024
        ),
    )(queries, key_rows, value_rows)


def solution(mesh):
    placed = (P("seq", "head"), P("seq", "head"), P("seq", "head"))
    return jax.shard_map(
        per_device, mesh=mesh, in_specs=placed, out_specs=P("seq", "head"), check_vma=False
    )
```

profile of v0, /device:TPU:0, one launch (start us, length us, event | category | flops | bytes accessed | tf_op | source)
XLA Modules:
  0.0 69.8 jit_solution(3827396898510887303)
XLA Ops:
  0.0 0.0 copy-start
  0.0 1.2 %copy-done = bf16[256,2048]{1,0:T(8,128)(2,1)S(1)} copy-done((bf16[256,2048]{1,0:T(8,128)(2,1)S(1)}, bf16[256,2048]{1,0:T(8,128)(2,1)}, u32[]{:S(2)}) %copy-start) | copy-done | bytes 1048600
  1.2 0.0 copy-start.1
  1.2 1.2 %copy-done.1 = bf16[256,2048]{1,0:T(8,128)(2,1)S(1)} copy-done((bf16[256,2048]{1,0:T(8,128)(2,1)S(1)}, bf16[256,2048]{1,0:T(8,128)(2,1)}, u32[]{:S(2)}) %copy-start.1) | copy-done | bytes 1048600
  2.5 0.0 copy-start.2
  2.5 1.2 %copy-done.2 = bf16[256,2048]{1,0:T(8,128)(2,1)S(1)} copy-done((bf16[256,2048]{1,0:T(8,128)(2,1)S(1)}, bf16[256,2048]{1,0:T(8,128)(2,1)}, u32[]{:S(2)}) %copy-start.2) | copy-done | bytes 1048600
  3.7 65.1 %shard_map.37 = bf16[256,2048]{1,0:T(8,128)(2,1)S(1)} custom-call(bf16[256,2048]{1,0:T(8,128)(2,1)S(1)} %copy-done, bf16[256,2048]{1,0:T(8,128)(2,1)S(1)} %copy-done.1, bf16[256,2048]{1,0:T(8,128)(2,1)S(1)} %copy-done.2), custom_call_target="tpu_custom_call" | custom-call | tf_op jit(solution)/shard_map/pallas_call | solution.py:362
  68.8 1.0 %copy.5 = bf16[256,2048]{1,0:T(8,128)(2,1)} copy(bf16[256,2048]{1,0:T(8,128)(2,1)S(1)} %shard_map.37) | data formatting | bytes 2097152
Async XLA Ops:
  0.0 1.2 %copy-start = (bf16[256,2048]{1,0:T(8,128)(2,1)S(1)}, bf16[256,2048]{1,0:T(8,128)(2,1)}, u32[]{:S(2)}) copy-start(bf16[256,2048]{1,0:T(8,128)(2,1)} %q_ref.1) | copy-start | bytes 3145732
  1.2 1.2 %copy-start.1 = (bf16[256,2048]{1,0:T(8,128)(2,1)S(1)}, bf16[256,2048]{1,0:T(8,128)(2,1)}, u32[]{:S(2)}) copy-start(bf16[256,2048]{1,0:T(8,128)(2,1)} %k_ref.1) | copy-start | bytes 3145732
  2.5 1.2 %copy-start.2 = (bf16[256,2048]{1,0:T(8,128)(2,1)S(1)}, bf16[256,2048]{1,0:T(8,128)(2,1)}, u32[]{:S(2)}) copy-start(bf16[256,2048]{1,0:T(8,128)(2,1)} %v_ref.1) | copy-start | bytes 3145732
where the time goes:
time: 70 us; the launch traced here: 69.8 us
  Pallas kernels  65.1 us (93%)
  local copies, waits for them, and re-layouts  4.65 us (7%)
    pallas_call x1, Pallas kernels, per_device(): pl.pallas_call(functools.partial(kernel, groups), out_shape=jax.ShapeDtyp...  65.1 us
    unnamed x7, local copies, waits for them, and re-layouts  4.65 us

commit v1 on v0

--- a/solution.py
+++ b/solution.py
@@ -25,31 +25,19 @@
 MID_LOW, MID_BLOCKS = -MID_REACH, GROUP_BLOCKS + 2 * MID_REACH
 FAR_LOW, FAR_BLOCKS = -FAR_REACH, GROUP_BLOCKS + 2 * FAR_REACH
 
-KIND_K, KIND_V, KIND_Q, KIND_O = 0, 1, 2, 3
-FIRST_HOP = (
-    (4, 1, "fine", 3, 1, -1),
-    (5, -1, "fine", 0, 1, 4),
-    (6, 1, "mid", 1, 2, -3),
-    (7, -1, "mid", 1, 2, 5),
-    (8, 1, "far", 0, 1, -4),
-    (9, -1, "far", 3, 1, 7),
+KIND_K, KIND_V, KIND_Q, KIND_O, KIND_EDGE_K, KIND_EDGE_V, KIND_FINE, KIND_MID_OWN = range(8)
+KIND_MID_OTHER, KIND_FAR = KIND_MID_OWN + 2, KIND_MID_OWN + 4
+SECOND_HOP = (
+    (13, 2, -4, 4, -8, 1),
+    (14, -2, 4, 4, 8, -1),
 )
-SECOND_HOP = (
-    (10, 2, "far", -4, 4, -8),
-    (11, -2, "far", 4, 4, 8),
+DIRECT = (
+    (15, 3, 3, 1, -9, 3),
+    (16, -3, 0, 1, 12, -3),
 )
-THIRD_HOP = (
-    (12, 3, "far", -5, 1, -9),
-    (13, -3, "far", 8, 1, 12),
-)
-ROUTES = FIRST_HOP + SECOND_HOP + THIRD_HOP
-RELAY_LAG, FORWARD_LAG, ATTEND_LAG = 2, 3, 4
-KINDS = 14
+RELAY_LAG, ATTEND_LAG = 3, 6
+KINDS = 17
 MESH = pl.DeviceIdType.MESH
-
-
-def hop_of(offset):
-    return 1 if offset > 0 else -1
 
 
 def pool_matrix(out_rows, in_rows, group_rows):
@@ -66,24 +54,28 @@
 def kernel(
     groups, q_ref, k_ref, v_ref, o_ref,
     q_rows, fine, mid, far, coarse, out_rows, bias,
-    send, recv, coarse_send, coarse_recv, local,
+    send, recv, coarse_send, coarse_recv, local, entered,
 ):
     me = lax.axis_index("seq")
     group = me // 2
     parity = me % 2
     partner = me + 1 - 2 * parity
+    outward = 2 * parity - 1
     rows_dev = q_ref.shape[0]
     chunks = q_rows.shape[0]
     half_cols = chunks * HEAD_DIM
     own_first = pl.multiple_of(parity * rows_dev, rows_dev)
     other_first = pl.multiple_of((1 - parity) * rows_dev, rows_dev)
-    levels = {"fine": (fine, BLOCK, FINE_LOW), "mid": (mid, HALF, MID_LOW), "far": (far, QUARTER, FAR_LOW)}
+    half_blocks = GROUP_BLOCKS // 2
 
     def own_cols(chunk):
         return pl.ds(pl.multiple_of(parity * half_cols + chunk * HEAD_DIM, HEAD_DIM), HEAD_DIM)
 
     def other_cols(chunk):
         return pl.ds(pl.multiple_of((1 - parity) * half_cols + chunk * HEAD_DIM, HEAD_DIM), HEAD_DIM)
+
+    def fine_rows(block):
+        return pl.ds(pl.multiple_of((block - FINE_LOW) * BLOCK, BLOCK), BLOCK)
 
     def remote(src, dst, kind, chunk, target):
         return pltpu.make_async_remote_copy(
@@ -108,13 +100,48 @@
             kind, chunk, partner,
         )
 
+    def edge_copy(side, chunk):
+        source = v_ref if side else k_ref
+        rows = pl.ds(pl.multiple_of(parity * (rows_dev - BLOCK), BLOCK), BLOCK)
+        landing = (1 - parity) * (GROUP_BLOCKS + 1) - 1
+        return remote(
+            source.at[rows, own_cols(chunk)], fine.at[chunk, side, fine_rows(landing)],
+            KIND_EDGE_K + side, chunk, me + 2 * outward,
+        )
+
+    def fine_copy(chunk):
+        first = (1 - parity) * (GROUP_BLOCKS - 1)
+        landing = parity * (GROUP_BLOCKS + 1) - 1
+        return remote(
+            fine.at[chunk, :, fine_rows(first)], fine.at[chunk, :, fine_rows(landing)],
+            KIND_FINE, chunk, me - 2 * outward,
+        )
+
+    def mid_rows(block):
+        return pl.ds(pl.multiple_of((block - MID_LOW) * HALF, HALF), HALF)
+
+    def far_rows(first, count):
+        return pl.ds((first - FAR_LOW) * QUARTER, count * QUARTER)
+
+    def mid_copy(other, way, chunk):
+        block = 2 - parity if other else 1 + parity
+        return remote(
+            mid.at[chunk, :, mid_rows(block)], mid.at[chunk, :, mid_rows(block - GROUP_BLOCKS * way)],
+            KIND_MID_OWN + 2 * other + (way < 0), chunk, me + 2 * way,
+        )
+
+    def far_copy(way, chunk):
+        first, landing = (0, -GROUP_BLOCKS) if way > 0 else (GROUP_BLOCKS - 1, 2 * GROUP_BLOCKS - 1)
+        return remote(
+            far.at[chunk, :, far_rows(first, 1)], far.at[chunk, :, far_rows(landing, 1)],
+            KIND_FAR + (way < 0), chunk, me + 2 * way,
+        )
+
     def routed(route, chunk):
-        kind, offset, level, first, count, landing = route
-        window, unit, low = levels[level]
+        kind, offset, first, count, landing, hop = route
         return remote(
-            window.at[chunk, :, pl.ds((first - low) * unit, count * unit)],
-            window.at[chunk, :, pl.ds((landing - low) * unit, count * unit)],
-            kind, chunk, me + 2 * hop_of(offset),
+            far.at[chunk, :, far_rows(first, count)], far.at[chunk, :, far_rows(landing, count)],
+            kind, chunk, me + 2 * hop,
         )
 
     def coarse_copy(chunk, step):
@@ -131,9 +158,7 @@
 
     def start_routes(routes, chunk):
         for route in routes:
-            hop = hop_of(route[1])
-
-            @pl.when(inside(hop) & inside(hop - route[1]))
+            @pl.when(inside(route[5]) & inside(route[5] - route[1]))
             def _():
                 routed(route, chunk).start()
 
@@ -157,31 +182,82 @@
             local.at[chunk, KIND_O],
         )
 
+    @pl.loop(0, chunks)
+    def _(chunk):
+        coarse[chunk] = jnp.zeros(coarse.shape[1:], jnp.bfloat16)
+
     barrier = pltpu.get_barrier_semaphore()
     pl.semaphore_signal(barrier, inc=1, device_id={"seq": partner}, device_id_type=MESH)
-
-    @pl.loop(1, groups)
-    def _(step):
-        target = lax.rem(group + step, groups) * 2 + parity
-        pl.semaphore_signal(barrier, inc=1, device_id={"seq": target}, device_id_type=MESH)
-
-    pl.semaphore_wait(barrier, groups)
+    for way in (1, -1):
+        @pl.when(inside(way))
+        def _():
+            pl.semaphore_signal(barrier, inc=1, device_id={"seq": me + 2 * way}, device_id_type=MESH)
+
+    pl.semaphore_wait(barrier, 1 + inside(1).astype(jnp.int32) + inside(-1).astype(jnp.int32))
 
     @pl.loop(0, chunks)
     def _(chunk):
+        own_copy(KIND_K, chunk).start()
+        own_copy(KIND_V, chunk).start()
         exchange(KIND_K, chunk).start()
         exchange(KIND_V, chunk).start()
-        own_copy(KIND_K, chunk).start()
-        own_copy(KIND_V, chunk).start()
+
+        @pl.when(inside(outward))
+        def _():
+            edge_copy(0, chunk).start()
+            edge_copy(1, chunk).start()
 
     @pl.loop(0, chunks)
     def _(chunk):
+        own_copy(KIND_Q, chunk).start()
         exchange(KIND_Q, chunk).start()
-        own_copy(KIND_Q, chunk).start()
-
-    for _, offset, level, _, count, landing in ROUTES:
-        window, unit, low = levels[level]
-
+
+    def pool_half(chunk, half):
+        first = half * rows_dev
+        for side in range(2):
+            rows = fine[chunk, side, pl.ds(pl.multiple_of(BLOCK + first, BLOCK), rows_dev)]
+            twos = pooled(rows, rows_dev // 2, 2)
+            fours = pooled(twos, rows_dev // 4, 2)
+            mid[chunk, side, pl.ds(pl.multiple_of(-MID_LOW * HALF + first // 2, HALF), rows_dev // 2)] = twos
+            far[chunk, side, pl.ds(pl.multiple_of(-FAR_LOW * QUARTER + first // 4, QUARTER), rows_dev // 4)] = fours
+
+    @pl.loop(0, chunks)
+    def _(chunk):
+        own_copy(KIND_K, chunk).wait()
+        own_copy(KIND_V, chunk).wait()
+        pool_half(chunk, parity)
+        for way in (-1, 1):
+            @pl.when(inside(way))
+            def _():
+                mid_copy(0, way, chunk).start()
+
+                @pl.when(outward == -way)
+                def _():
+                    far_copy(way, chunk).start()
+
+    for way in (1, -1):
+        @pl.when(inside(-way))
+        def _():
+            pl.semaphore_wait(entered.at[(1 - way) // 2], 1)
+
+        @pl.when(inside(way))
+        def _():
+            pl.semaphore_signal(
+                entered.at[(1 - way) // 2], inc=1, device_id={"seq": me + 2 * way}, device_id_type=MESH
+            )
+
+    for window, unit, low, offset, landing, count in (
+        (fine, BLOCK, FINE_LOW, 1, -1, 1),
+        (fine, BLOCK, FINE_LOW, -1, 4, 1),
+        (mid, HALF, MID_LOW, 1, -3, 2),
+        (mid, HALF, MID_LOW, -1, 5, 2),
+        (far, QUARTER, FAR_LOW, 1, -4, 1),
+        (far, QUARTER, FAR_LOW, -1, 7, 1),
+        (far, QUARTER, FAR_LOW, 2, -8, 4),
+        (far, QUARTER, FAR_LOW, -2, 8, 4),
+        (far, QUARTER, FAR_LOW, 3, -9, 1),
+        (far, QUARTER, FAR_LOW, -3, 12, 1),
+    ):
         @pl.when(jnp.logical_not(inside(-offset)))
         def _():
             @pl.loop(0, chunks)
@@ -228,18 +304,27 @@
 
     def gather(chunk):
         for kind in (KIND_K, KIND_V):
-            own_copy(kind, chunk).wait()
             exchange(kind, chunk).wait_recv()
-        start_routes(FIRST_HOP[:2], chunk)
+
+        @pl.when(inside(-outward))
+        def _():
+            fine_copy(chunk).start()
+
+        pool_half(chunk, 1 - parity)
         slot = pl.ds(pl.multiple_of(group * COARSE_SLOT, COARSE_SLOT), COARSE_SLOT)
         for side in range(2):
-            rows = fine[chunk, side, BLOCK : BLOCK + GROUP_ROWS]
-            twos = pooled(rows, GROUP_ROWS // 2, 2)
-            fours = pooled(twos, GROUP_ROWS // 4, 2)
-            mid[chunk, side, -MID_LOW * HALF : (GROUP_BLOCKS - MID_LOW) * HALF] = twos
-            far[chunk, side, -FAR_LOW * QUARTER : (GROUP_BLOCKS - FAR_LOW) * QUARTER] = fours
+            fours = far[chunk, side, -FAR_LOW * QUARTER : (GROUP_BLOCKS - FAR_LOW) * QUARTER]
             coarse[chunk, side, slot] = pooled(fours, COARSE_SLOT, POOL // 4)
-        start_routes(FIRST_HOP[2:], chunk)
+        for way in (-1, 1):
+            @pl.when(inside(way))
+            def _():
+                mid_copy(1, way, chunk).start()
+
+                @pl.when(outward == way)
+                def _():
+                    far_copy(way, chunk).start()
+
+        start_routes(DIRECT, chunk)
 
         @pl.loop(1, groups)
         def _(step):
@@ -248,28 +333,44 @@
                 coarse_copy(chunk, step).start()
 
     def relay(chunk):
-        await_routes(FIRST_HOP, chunk)
+        @pl.when(inside(-outward))
+        def _():
+            edge_copy(0, chunk).wait_recv()
+            edge_copy(1, chunk).wait_recv()
+
+        @pl.when(inside(outward))
+        def _():
+            fine_copy(chunk).wait_recv()
+
+        for way in (-1, 1):
+            @pl.when(inside(-way))
+            def _():
+                mid_copy(0, way, chunk).wait_recv()
+                mid_copy(1, way, chunk).wait_recv()
+                far_copy(way, chunk).wait_recv()
+
         for side in range(2):
-            mid[chunk, side, 2 * HALF : 3 * HALF] = pooled(fine[chunk, side, :BLOCK], HALF, 2)
-            mid[chunk, side, 7 * HALF : 8 * HALF] = pooled(fine[chunk, side, 5 * BLOCK :], HALF, 2)
+            below = pooled(fine[chunk, side, :BLOCK], HALF, 2)
+            above = pooled(fine[chunk, side, 5 * BLOCK :], HALF, 2)
+            mid[chunk, side, 2 * HALF : 3 * HALF] = below
+            mid[chunk, side, 7 * HALF : 8 * HALF] = above
             far[chunk, side, 6 * QUARTER : 9 * QUARTER] = pooled(
-                mid[chunk, side, : 3 * HALF], 3 * QUARTER, 2
+                jnp.concatenate([mid[chunk, side, : 2 * HALF], below], axis=0), 3 * QUARTER, 2
             )
             far[chunk, side, 13 * QUARTER : 16 * QUARTER] = pooled(
-                mid[chunk, side, 7 * HALF :], 3 * QUARTER, 2
+                jnp.concatenate([above, mid[chunk, side, 8 * HALF :]], axis=0), 3 * QUARTER, 2
             )
         start_routes(SECOND_HOP, chunk)
 
-    def forward(chunk):
-        await_routes(SECOND_HOP, chunk)
-        start_routes(THIRD_HOP, chunk)
-
     scale = math.log2(math.e) / math.sqrt(HEAD_DIM)
+
+    def rows_at(ref, chunk, side, first, count, unit):
+        return ref[chunk, side, pl.ds(pl.multiple_of(first * unit, unit), count * unit)]
 
     def attend(chunk):
         own_copy(KIND_Q, chunk).wait()
         exchange(KIND_Q, chunk).wait_recv()
-        await_routes(THIRD_HOP, chunk)
+        await_routes(SECOND_HOP + DIRECT, chunk)
 
         @pl.loop(1, groups)
         def _(step):
@@ -284,7 +385,7 @@
                     device_id={"seq": partner}, device_id_type=MESH,
                 ).wait_recv()
 
-        for offset in (-2, -1, 1, 2):
+        for offset in (-2, 2):
             @pl.when(inside(offset))
             def _():
                 near = pl.ds(pl.multiple_of((group + offset) * COARSE_SLOT, COARSE_SLOT), COARSE_SLOT)
@@ -293,22 +394,23 @@
                     fours = far[chunk, side, first : first + GROUP_ROWS // 4]
                     coarse[chunk, side, near] = pooled(fours, COARSE_SLOT, POOL // 4)
 
-        for block in range(GROUP_BLOCKS):
+        def attend_block(block):
             def atom_rows(side):
                 return jnp.concatenate(
                     [
-                        fine[chunk, side, block * BLOCK : (block + 3) * BLOCK],
-                        mid[chunk, side, block * HALF : (block + 2) * HALF],
-                        mid[chunk, side, (block + 5) * HALF : (block + 7) * HALF],
-                        far[chunk, side, block * QUARTER : (block + 6) * QUARTER],
-                        far[chunk, side, (block + 13) * QUARTER : (block + 19) * QUARTER],
+                        rows_at(fine, chunk, side, block, 3, BLOCK),
+                        rows_at(mid, chunk, side, block, 2, HALF),
+                        rows_at(mid, chunk, side, block + 5, 2, HALF),
+                        rows_at(far, chunk, side, block, 6, QUARTER),
+                        rows_at(far, chunk, side, block + 13, 6, QUARTER),
                         coarse[chunk, side],
                     ],
                     axis=0,
                 )
 
+            here = pl.ds(pl.multiple_of(block * BLOCK, BLOCK), BLOCK)
             scores = lax.dot_general(
-                q_rows[chunk, block * BLOCK : (block + 1) * BLOCK], atom_rows(0),
+                q_rows[chunk, here], atom_rows(0),
                 (((1,), (1,)), ((), ())), preferred_element_type=jnp.float32,
             ) * scale + bias[pl.ds(block, 1), :]
             row_top = jnp.max(scores, axis=1, keepdims=True)
@@ -317,13 +419,16 @@
             weighted = jnp.dot(
                 exp_terms.astype(jnp.bfloat16), atom_rows(1), preferred_element_type=jnp.float32
             )
-            out_rows[chunk, block * BLOCK : (block + 1) * BLOCK] = (weighted / denominator).astype(
-                jnp.bfloat16
-            )
+            out_rows[chunk, here] = (weighted / denominator).astype(jnp.bfloat16)
+
+        for block in range(half_blocks):
+            attend_block((1 - parity) * half_blocks + block)
         exchange(KIND_O, chunk).start()
+        for block in range(half_blocks):
+            attend_block(parity * half_blocks + block)
         own_result(chunk).start()
 
-    stages = ((gather, 0), (relay, RELAY_LAG), (forward, FORWARD_LAG), (attend, ATTEND_LAG))
+    stages = ((gather, 0), (relay, RELAY_LAG), (attend, ATTEND_LAG))
 
     @pl.loop(0, chunks + ATTEND_LAG)
     def _(step):
@@ -338,10 +443,25 @@
         exchange(KIND_O, chunk).wait_recv()
         for kind in (KIND_K, KIND_V, KIND_Q, KIND_O):
             exchange(kind, chunk).wait_send()
-        for route in ROUTES:
-            hop = hop_of(route[1])
-
-            @pl.when(inside(hop) & inside(hop - route[1]))
+
+        @pl.when(inside(outward))
+        def _():
+            edge_copy(0, chunk).wait_send()
+            edge_copy(1, chunk).wait_send()
+
+        @pl.when(inside(-outward))
+        def _():
+            fine_copy(chunk).wait_send()
+
+        for way in (-1, 1):
+            @pl.when(inside(way))
+            def _():
+                mid_copy(0, way, chunk).wait_send()
+                mid_copy(1, way, chunk).wait_send()
+                far_copy(way, chunk).wait_send()
+
+        for route in SECOND_HOP + DIRECT:
+            @pl.when(inside(route[5]) & inside(route[5] - route[1]))
             def _():
                 routed(route, chunk).wait_send()
 
@@ -377,11 +497,12 @@
             pltpu.SemaphoreType.DMA((chunks, groups)),
             pltpu.SemaphoreType.DMA((chunks, groups)),
             pltpu.SemaphoreType.DMA((chunks, 4)),
+            pltpu.SemaphoreType.REGULAR((2,)),
         ],
         compiler_params=pltpu.CompilerParams(
             collective_id=0, has_side_effects=True, vmem_limit_bytes=48 * 1024 * 1024
         ),
-    )(queries, key_rows, value_rows)
+    )(*(pltpu.with_memory_space_constraint(source, pltpu.HBM) for source in (queries, key_rows, value_rows)))
 
 
 def solution(mesh):

time: 70 us -> 60.3 us (0.86)
  Pallas kernels: 65.1 us -> 59.1 us
  local copies, waits for them, and re-layouts: 4.65 us -> 0.97 us
    pallas_call x1, Pallas kernels: 65.1 us -> 59.1 us  [per_device(): pl.pallas_call(functools.partial(kernel, groups), out_shape=jax.ShapeDtyp...]
    unnamed x7 -> x1, local copies, waits for them, and re-layouts: 4.65 us -> 0.97 us
where the time goes in v1:
time: 60.3 us; the launch traced here: 60.1 us
  Pallas kernels  59.1 us (98%)
  local copies, waits for them, and re-layouts  0.97 us (2%)
    pallas_call x1, Pallas kernels, per_device(): pl.pallas_call(functools.partial(kernel, groups), out_shape=jax.ShapeDtyp...  59.1 us

profile of v1, /device:TPU:0, one launch (start us, length us, event | category | flops | bytes accessed | tf_op | source)
XLA Modules:
  0.0 60.1 jit_solution(7097430436171890096)
XLA Ops:
  0.0 59.1 %shard_map.37 = bf16[256,2048]{1,0:T(8,128)(2,1)S(1)} custom-call(bf16[256,2048]{1,0:T(8,128)(2,1)} %q_ref.1, bf16[256,2048]{1,0:T(8,128)(2,1)} %k_ref.1, bf16[256,2048]{1,0:T(8,128)(2,1)} %v_ref.1), custom_call_target="tpu_custom_call" | custom-call | tf_op jit(solution)/shard_map/pallas_call | solution.py:482
  59.2 1.0 %copy.5 = bf16[256,2048]{1,0:T(8,128)(2,1)} copy(bf16[256,2048]{1,0:T(8,128)(2,1)S(1)} %shard_map.37) | data formatting | bytes 2097152

commit v2 on v1

--- a/solution.py
+++ b/solution.py
@@ -35,8 +35,11 @@
     (15, 3, 3, 1, -9, 3),
     (16, -3, 0, 1, 12, -3),
 )
-RELAY_LAG, ATTEND_LAG = 3, 6
-KINDS = 17
+RELAY_LAG, ATTEND_LAG = 2, 4
+AHEAD, QUERY_LAG = 4, 1
+STAGES = 4
+KINDS = 18
+KIND_LAST = 17
 MESH = pl.DeviceIdType.MESH
 
 
@@ -54,7 +57,7 @@
 def kernel(
     groups, q_ref, k_ref, v_ref, o_ref,
     q_rows, fine, mid, far, coarse, out_rows, bias,
-    send, recv, coarse_send, coarse_recv, local, entered,
+    stage, send, recv, coarse_send, coarse_recv, local, entered,
 ):
     me = lax.axis_index("seq")
     group = me // 2
@@ -89,15 +92,17 @@
                 q_ref.at[:, other_cols(chunk)], q_rows.at[chunk, pl.ds(own_first, rows_dev)],
                 kind, chunk, partner,
             )
-        if kind == KIND_O:
-            return remote(
-                out_rows.at[chunk, pl.ds(other_first, rows_dev)], o_ref.at[:, own_cols(chunk)],
-                kind, chunk, partner,
-            )
         source = k_ref if kind == KIND_K else v_ref
         return remote(
             source.at[:, other_cols(chunk)], fine.at[chunk, kind, pl.ds(BLOCK + own_first, rows_dev)],
             kind, chunk, partner,
+        )
+
+    def result_copy(step, chunk):
+        source = out_rows.at[chunk, pl.ds(pl.multiple_of(other_first + step * BLOCK, BLOCK), BLOCK)]
+        return remote(
+            source, o_ref.at[step * BLOCK : (step + 1) * BLOCK, own_cols(chunk)], KIND_O + step * (KIND_LAST - KIND_O),
+            chunk, partner,
         )
 
     def edge_copy(side, chunk):
@@ -186,6 +191,12 @@
     def _(chunk):
         coarse[chunk] = jnp.zeros(coarse.shape[1:], jnp.bfloat16)
 
+    def start_edge(chunk):
+        @pl.when(inside(outward))
+        def _():
+            edge_copy(0, chunk).start()
+            edge_copy(1, chunk).start()
+
     barrier = pltpu.get_barrier_semaphore()
     pl.semaphore_signal(barrier, inc=1, device_id={"seq": partner}, device_id_type=MESH)
     for way in (1, -1):
@@ -202,27 +213,46 @@
         exchange(KIND_K, chunk).start()
         exchange(KIND_V, chunk).start()
 
-        @pl.when(inside(outward))
-        def _():
-            edge_copy(0, chunk).start()
-            edge_copy(1, chunk).start()
+        @pl.when(chunk < AHEAD)
+        def _():
+            start_edge(chunk)
+
+        @pl.when(chunk >= QUERY_LAG)
+        def _():
+            exchange(KIND_Q, chunk - QUERY_LAG).start()
 
     @pl.loop(0, chunks)
     def _(chunk):
         own_copy(KIND_Q, chunk).start()
-        exchange(KIND_Q, chunk).start()
-
-    def pool_half(chunk, half):
+
+        @pl.when(chunk >= chunks - QUERY_LAG)
+        def _():
+            exchange(KIND_Q, chunk).start()
+
+    def paired(slot, first, rows, stride, step):
+        low = stage[slot, pl.ds(first + step, rows, stride=stride)]
+        high = stage[slot, pl.ds(first + step + 1, rows, stride=stride)]
+        return (0.5 * (low + high)).astype(jnp.bfloat16)
+
+    def twos_of(slot, first, rows):
+        return paired(slot, first, rows // 2, 2, 0)
+
+    def fours_of(slot, first, rows):
+        low, high = (paired(slot, first, rows // 4, 4, step).astype(jnp.float32) for step in (0, 2))
+        return (0.5 * (low + high)).astype(jnp.bfloat16)
+
+    def pool_half(chunk, half, base=0):
         first = half * rows_dev
         for side in range(2):
             rows = fine[chunk, side, pl.ds(pl.multiple_of(BLOCK + first, BLOCK), rows_dev)]
-            twos = pooled(rows, rows_dev // 2, 2)
-            fours = pooled(twos, rows_dev // 4, 2)
+            stage[base + side] = rows.astype(jnp.float32)
+        for side in range(2):
+            twos = twos_of(base + side, 0, rows_dev)
             mid[chunk, side, pl.ds(pl.multiple_of(-MID_LOW * HALF + first // 2, HALF), rows_dev // 2)] = twos
+            fours = fours_of(base + side, 0, rows_dev)
             far[chunk, side, pl.ds(pl.multiple_of(-FAR_LOW * QUARTER + first // 4, QUARTER), rows_dev // 4)] = fours
 
-    @pl.loop(0, chunks)
-    def _(chunk):
+    def prepare(chunk):
         own_copy(KIND_K, chunk).wait()
         own_copy(KIND_V, chunk).wait()
         pool_half(chunk, parity)
@@ -234,6 +264,10 @@
                 @pl.when(outward == -way)
                 def _():
                     far_copy(way, chunk).start()
+
+    @pl.loop(0, AHEAD)
+    def _(chunk):
+        prepare(chunk)
 
     for way in (1, -1):
         @pl.when(inside(-way))
@@ -292,15 +326,22 @@
         held = (here >= 0) & (here < total_blocks)
         late = place - windows_end
         slot_row = late % COARSE_SLOT
-        coarse_block = late // COARSE_SLOT * GROUP_BLOCKS + slot_row * POOL // BLOCK
+        slot = late // COARSE_SLOT
+        giver = jnp.where(slot < 2, group + 4 * slot - 2, slot - 2)
+        given = (giver >= 0) & (giver < groups) & ((slot < 2) | (jnp.abs(giver - group) > 2))
+        coarse_block = giver * GROUP_BLOCKS + slot_row * POOL // BLOCK
         apart = jnp.abs(coarse_block - (group * GROUP_BLOCKS + block)) > FAR_REACH
         allowed = ((place < windows_end) & held) | (
-            (place >= windows_end) & (slot_row < COARSE_USED) & apart
+            (place >= windows_end) & (slot_row < COARSE_USED) & given & apart
         )
         log_size = jnp.where(
             place < 384, 0.0, jnp.where(place < 640, 1.0, jnp.where(place < windows_end, 2.0, math.log2(POOL)))
         )
         bias[pl.ds(block, 1), :] = jnp.where(allowed, log_size, -jnp.inf)
+
+    def near_coarse(chunk, side, offset):
+        first = (offset * GROUP_BLOCKS - FAR_LOW) * QUARTER
+        return pooled(far[chunk, side, first : first + GROUP_ROWS // 4], COARSE_SLOT, POOL // 4)
 
     def gather(chunk):
         for kind in (KIND_K, KIND_V):
@@ -311,10 +352,6 @@
             fine_copy(chunk).start()
 
         pool_half(chunk, 1 - parity)
-        slot = pl.ds(pl.multiple_of(group * COARSE_SLOT, COARSE_SLOT), COARSE_SLOT)
-        for side in range(2):
-            fours = far[chunk, side, -FAR_LOW * QUARTER : (GROUP_BLOCKS - FAR_LOW) * QUARTER]
-            coarse[chunk, side, slot] = pooled(fours, COARSE_SLOT, POOL // 4)
         for way in (-1, 1):
             @pl.when(inside(way))
             def _():
@@ -326,11 +363,17 @@
 
         start_routes(DIRECT, chunk)
 
-        @pl.loop(1, groups)
-        def _(step):
-            @pl.when(jnp.abs(lax.rem(group + step, groups) - group) > 2)
-            def _():
-                coarse_copy(chunk, step).start()
+        @pl.when(inside(3) | inside(-3))
+        def _():
+            slot = pl.ds(pl.multiple_of(group * COARSE_SLOT, COARSE_SLOT), COARSE_SLOT)
+            for side in range(2):
+                coarse[chunk, side, slot] = near_coarse(chunk, side, 0)
+
+            @pl.loop(1, groups)
+            def _(step):
+                @pl.when(jnp.abs(lax.rem(group + step, groups) - group) > 2)
+                def _():
+                    coarse_copy(chunk, step).start()
 
     def relay(chunk):
         @pl.when(inside(-outward))
@@ -350,16 +393,16 @@
                 far_copy(way, chunk).wait_recv()
 
         for side in range(2):
-            below = pooled(fine[chunk, side, :BLOCK], HALF, 2)
-            above = pooled(fine[chunk, side, 5 * BLOCK :], HALF, 2)
-            mid[chunk, side, 2 * HALF : 3 * HALF] = below
-            mid[chunk, side, 7 * HALF : 8 * HALF] = above
-            far[chunk, side, 6 * QUARTER : 9 * QUARTER] = pooled(
-                jnp.concatenate([mid[chunk, side, : 2 * HALF], below], axis=0), 3 * QUARTER, 2
-            )
-            far[chunk, side, 13 * QUARTER : 16 * QUARTER] = pooled(
-                jnp.concatenate([above, mid[chunk, side, 8 * HALF :]], axis=0), 3 * QUARTER, 2
-            )
+            for end, near_mid in ((0, 0), (GROUP_BLOCKS + 1, GROUP_BLOCKS + MID_REACH + 1)):
+                slot = 2 * side + (end > 0)
+                stage[slot, :BLOCK] = fine[chunk, side, end * BLOCK : (end + 1) * BLOCK].astype(jnp.float32)
+                stage[slot, BLOCK:] = mid[chunk, side, near_mid * HALF : (near_mid + 2) * HALF].astype(jnp.float32)
+        for side in range(2):
+            for end, one, two in ((0, -1, -3), (1, GROUP_BLOCKS, GROUP_BLOCKS + 1)):
+                slot = 2 * side + end
+                mid[chunk, side, mid_rows(one)] = twos_of(slot, 0, BLOCK)
+                far[chunk, side, far_rows(one, 1)] = fours_of(slot, 0, BLOCK)
+                far[chunk, side, far_rows(two, 2)] = twos_of(slot, BLOCK, BLOCK)
         start_routes(SECOND_HOP, chunk)
 
     scale = math.log2(math.e) / math.sqrt(HEAD_DIM)
@@ -372,63 +415,73 @@
         exchange(KIND_Q, chunk).wait_recv()
         await_routes(SECOND_HOP + DIRECT, chunk)
 
-        @pl.loop(1, groups)
-        def _(step):
-            giver = lax.rem(group - step + groups, groups)
-            origin = pl.ds(pl.multiple_of(giver * COARSE_SLOT, COARSE_SLOT), COARSE_SLOT)
-
-            @pl.when(jnp.abs(giver - group) > 2)
-            def _():
-                pltpu.make_async_remote_copy(
-                    src_ref=coarse.at[chunk, :, origin], dst_ref=coarse.at[chunk, :, origin],
-                    send_sem=coarse_send.at[chunk, step], recv_sem=coarse_recv.at[chunk, step],
-                    device_id={"seq": partner}, device_id_type=MESH,
-                ).wait_recv()
-
-        for offset in (-2, 2):
-            @pl.when(inside(offset))
-            def _():
-                near = pl.ds(pl.multiple_of((group + offset) * COARSE_SLOT, COARSE_SLOT), COARSE_SLOT)
-                first = (offset * GROUP_BLOCKS - FAR_LOW) * QUARTER
-                for side in range(2):
-                    fours = far[chunk, side, first : first + GROUP_ROWS // 4]
-                    coarse[chunk, side, near] = pooled(fours, COARSE_SLOT, POOL // 4)
-
-        def attend_block(block):
-            def atom_rows(side):
-                return jnp.concatenate(
-                    [
-                        rows_at(fine, chunk, side, block, 3, BLOCK),
-                        rows_at(mid, chunk, side, block, 2, HALF),
-                        rows_at(mid, chunk, side, block + 5, 2, HALF),
-                        rows_at(far, chunk, side, block, 6, QUARTER),
-                        rows_at(far, chunk, side, block + 13, 6, QUARTER),
-                        coarse[chunk, side],
-                    ],
-                    axis=0,
-                )
-
+        @pl.when(inside(3) | inside(-3))
+        def _():
+            @pl.loop(1, groups)
+            def _(step):
+                giver = lax.rem(group - step + groups, groups)
+                origin = pl.ds(pl.multiple_of(giver * COARSE_SLOT, COARSE_SLOT), COARSE_SLOT)
+
+                @pl.when(jnp.abs(giver - group) > 2)
+                def _():
+                    pltpu.make_async_remote_copy(
+                        src_ref=coarse.at[chunk, :, origin], dst_ref=coarse.at[chunk, :, origin],
+                        send_sem=coarse_send.at[chunk, step], recv_sem=coarse_recv.at[chunk, step],
+                        device_id={"seq": partner}, device_id_type=MESH,
+                    ).wait_recv()
+
+        near = [[near_coarse(chunk, side, offset) for offset in (-2, 2)] for side in range(2)]
+
+        def atom_rows(block, side):
+            return jnp.concatenate(
+                [
+                    rows_at(fine, chunk, side, block, 3, BLOCK),
+                    rows_at(mid, chunk, side, block, 2, HALF),
+                    rows_at(mid, chunk, side, block + 5, 2, HALF),
+                    rows_at(far, chunk, side, block, 6, QUARTER),
+                    rows_at(far, chunk, side, block + 13, 6, QUARTER),
+                    *near[side],
+                    coarse[chunk, side],
+                ],
+                axis=0,
+            )
+
+        def score_block(block):
             here = pl.ds(pl.multiple_of(block * BLOCK, BLOCK), BLOCK)
-            scores = lax.dot_general(
-                q_rows[chunk, here], atom_rows(0),
+            return lax.dot_general(
+                q_rows[chunk, here], atom_rows(block, 0),
                 (((1,), (1,)), ((), ())), preferred_element_type=jnp.float32,
             ) * scale + bias[pl.ds(block, 1), :]
+
+        def finish_block(block, scores):
+            here = pl.ds(pl.multiple_of(block * BLOCK, BLOCK), BLOCK)
             row_top = jnp.max(scores, axis=1, keepdims=True)
             exp_terms = jnp.exp2(scores - row_top)
             denominator = jnp.sum(exp_terms, axis=1, keepdims=True)
             weighted = jnp.dot(
-                exp_terms.astype(jnp.bfloat16), atom_rows(1), preferred_element_type=jnp.float32
+                exp_terms.astype(jnp.bfloat16), atom_rows(block, 1), preferred_element_type=jnp.float32
             )
             out_rows[chunk, here] = (weighted / denominator).astype(jnp.bfloat16)
 
-        for block in range(half_blocks):
-            attend_block((1 - parity) * half_blocks + block)
-        exchange(KIND_O, chunk).start()
-        for block in range(half_blocks):
-            attend_block(parity * half_blocks + block)
+        theirs = [(1 - parity) * half_blocks + step for step in range(half_blocks)]
+        ours = [parity * half_blocks + step for step in range(half_blocks)]
+        order = theirs + ours
+        scores = score_block(order[0])
+        for step in range(GROUP_BLOCKS):
+            later = score_block(order[step + 1]) if step + 1 < GROUP_BLOCKS else None
+            finish_block(order[step], scores)
+            scores = later
+            if step < half_blocks:
+                result_copy(step, chunk).start()
         own_result(chunk).start()
 
-    stages = ((gather, 0), (relay, RELAY_LAG), (attend, ATTEND_LAG))
+    def look_ahead(chunk):
+        @pl.when(chunk + AHEAD < chunks)
+        def _():
+            start_edge(chunk + AHEAD)
+            prepare(chunk + AHEAD)
+
+    stages = ((look_ahead, 0), (gather, 0), (relay, RELAY_LAG), (attend, ATTEND_LAG))
 
     @pl.loop(0, chunks + ATTEND_LAG)
     def _(step):
@@ -439,9 +492,7 @@
 
     @pl.loop(0, chunks)
     def _(chunk):
-        own_result(chunk).wait()
-        exchange(KIND_O, chunk).wait_recv()
-        for kind in (KIND_K, KIND_V, KIND_Q, KIND_O):
+        for kind in (KIND_K, KIND_V, KIND_Q):
             exchange(kind, chunk).wait_send()
 
         @pl.when(inside(outward))
@@ -470,13 +521,20 @@
             @pl.when(jnp.abs(lax.rem(group + step, groups) - group) > 2)
             def _():
                 coarse_copy(chunk, step).wait_send()
+
+    @pl.loop(0, chunks)
+    def _(chunk):
+        own_result(chunk).wait()
+        for step in range(half_blocks):
+            result_copy(step, chunk).wait_send()
+            result_copy(step, chunk).wait_recv()
 
 
 def per_device(queries, key_rows, value_rows):
     rows_dev, cols = queries.shape
     groups = lax.axis_size("seq") // 2
     chunks = cols // 2 // HEAD_DIM
-    atoms = 8 * BLOCK + groups * COARSE_SLOT
+    atoms = 8 * BLOCK + (groups + 2) * COARSE_SLOT
     bf16 = jnp.bfloat16
     placed = pl.BlockSpec(memory_space=pltpu.HBM)
     return pl.pallas_call(
@@ -492,6 +550,7 @@
             pltpu.VMEM((chunks, 2, groups * COARSE_SLOT, HEAD_DIM), bf16),
             pltpu.VMEM((chunks, 2 * rows_dev, HEAD_DIM), bf16),
             pltpu.VMEM((8, atoms), jnp.float32),
+            pltpu.VMEM((STAGES, rows_dev, HEAD_DIM), jnp.float32),
             pltpu.SemaphoreType.DMA((chunks, KINDS)),
             pltpu.SemaphoreType.DMA((chunks, KINDS)),
             pltpu.SemaphoreType.DMA((chunks, groups)),

time: 60.3 us -> 57.8 us (0.959)
  Pallas kernels: 59.1 us -> 56.7 us
    pallas_call x1, Pallas kernels: 59.1 us -> 56.7 us  [per_device(): pl.pallas_call(functools.partial(kernel, groups), out_shape=jax.ShapeDtyp...]
where the time goes in v2:
time: 57.8 us; the launch traced here: 57.7 us
  Pallas kernels  56.7 us (98%)
  local copies, waits for them, and re-layouts  0.97 us (2%)
    pallas_call x1, Pallas kernels, per_device(): pl.pallas_call(functools.partial(kernel, groups), out_shape=jax.ShapeDtyp...  56.7 us

profile of v2, /device:TPU:0, one launch (start us, length us, event | category | flops | bytes accessed | tf_op | source)
XLA Modules:
  0.0 57.7 jit_solution(791189389456685287)
XLA Ops:
  0.0 56.7 %shard_map.37 = bf16[256,2048]{1,0:T(8,128)(2,1)S(1)} custom-call(bf16[256,2048]{1,0:T(8,128)(2,1)} %q_ref.1, bf16[256,2048]{1,0:T(8,128)(2,1)} %k_ref.1, bf16[256,2048]{1,0:T(8,128)(2,1)} %v_ref.1), custom_call_target="tpu_custom_call" | custom-call | tf_op jit(solution)/shard_map/pallas_call | solution.py:540
  56.7 1.0 %copy.5 = bf16[256,2048]{1,0:T(8,128)(2,1)} copy(bf16[256,2048]{1,0:T(8,128)(2,1)S(1)} %shard_map.37) | data formatting | bytes 2097152

commit v3 on v2

--- a/solution.py
+++ b/solution.py
@@ -36,7 +36,7 @@
     (16, -3, 0, 1, 12, -3),
 )
 RELAY_LAG, ATTEND_LAG = 2, 4
-AHEAD, QUERY_LAG = 4, 1
+AHEAD, QUERY_LAG = 5, 1
 STAGES = 4
 KINDS = 18
 KIND_LAST = 17
@@ -149,12 +149,12 @@
             kind, chunk, me + 2 * hop,
         )
 
-    def coarse_copy(chunk, step):
+    def coarse_copy(pair, step):
         target = lax.rem(group + step, groups) * 2 + parity
         slot = pl.ds(pl.multiple_of(group * COARSE_SLOT, COARSE_SLOT), COARSE_SLOT)
         return pltpu.make_async_remote_copy(
-            src_ref=coarse.at[chunk, :, slot], dst_ref=coarse.at[chunk, :, slot],
-            send_sem=coarse_send.at[chunk, step], recv_sem=coarse_recv.at[chunk, step],
+            src_ref=coarse.at[pair, :, slot], dst_ref=coarse.at[pair, :, slot],
+            send_sem=coarse_send.at[pair, step], recv_sem=coarse_recv.at[pair, step],
             device_id={"seq": target}, device_id_type=MESH,
         )
 
@@ -187,9 +187,9 @@
             local.at[chunk, KIND_O],
         )
 
-    @pl.loop(0, chunks)
-    def _(chunk):
-        coarse[chunk] = jnp.zeros(coarse.shape[1:], jnp.bfloat16)
+    @pl.loop(0, coarse.shape[0])
+    def _(pair):
+        coarse[pair] = jnp.zeros(coarse.shape[1:], jnp.bfloat16)
 
     def start_edge(chunk):
         @pl.when(inside(outward))
@@ -329,15 +329,17 @@
         slot = late // COARSE_SLOT
         giver = jnp.where(slot < 2, group + 4 * slot - 2, slot - 2)
         given = (giver >= 0) & (giver < groups) & ((slot < 2) | (jnp.abs(giver - group) > 2))
-        coarse_block = giver * GROUP_BLOCKS + slot_row * POOL // BLOCK
+        coarse_block = giver * GROUP_BLOCKS + slot_row % COARSE_USED * POOL // BLOCK
         apart = jnp.abs(coarse_block - (group * GROUP_BLOCKS + block)) > FAR_REACH
-        allowed = ((place < windows_end) & held) | (
-            (place >= windows_end) & (slot_row < COARSE_USED) & given & apart
-        )
         log_size = jnp.where(
             place < 384, 0.0, jnp.where(place < 640, 1.0, jnp.where(place < windows_end, 2.0, math.log2(POOL)))
         )
-        bias[pl.ds(block, 1), :] = jnp.where(allowed, log_size, -jnp.inf)
+        for odd in range(2):
+            used = slot_row // COARSE_USED == jnp.where(slot < 2, 0, odd)
+            allowed = ((place < windows_end) & held) | ((place >= windows_end) & used & given & apart)
+            bias[odd * GROUP_BLOCKS + block : odd * GROUP_BLOCKS + block + 1, :] = jnp.where(
+                allowed, log_size, -jnp.inf
+            )
 
     def near_coarse(chunk, side, offset):
         first = (offset * GROUP_BLOCKS - FAR_LOW) * QUARTER
@@ -363,17 +365,20 @@
 
         start_routes(DIRECT, chunk)
 
-        @pl.when(inside(3) | inside(-3))
+        @pl.when((inside(3) | inside(-3)) & (chunk % 2 == 1))
         def _():
             slot = pl.ds(pl.multiple_of(group * COARSE_SLOT, COARSE_SLOT), COARSE_SLOT)
+            pair = chunk // 2
+            own = far_rows(0, GROUP_BLOCKS)
             for side in range(2):
-                coarse[chunk, side, slot] = near_coarse(chunk, side, 0)
+                fours = jnp.concatenate([far[chunk - 1, side, own], far[chunk, side, own]], axis=0)
+                coarse[pair, side, slot] = pooled(fours, COARSE_SLOT, POOL // 4)
 
             @pl.loop(1, groups)
             def _(step):
                 @pl.when(jnp.abs(lax.rem(group + step, groups) - group) > 2)
                 def _():
-                    coarse_copy(chunk, step).start()
+                    coarse_copy(pair, step).start()
 
     def relay(chunk):
         @pl.when(inside(-outward))
@@ -415,7 +420,9 @@
         exchange(KIND_Q, chunk).wait_recv()
         await_routes(SECOND_HOP + DIRECT, chunk)
 
-        @pl.when(inside(3) | inside(-3))
+        pair = chunk // 2
+
+        @pl.when((inside(3) | inside(-3)) & (chunk % 2 == 0))
         def _():
             @pl.loop(1, groups)
             def _(step):
@@ -425,8 +432,8 @@
                 @pl.when(jnp.abs(giver - group) > 2)
                 def _():
                     pltpu.make_async_remote_copy(
-                        src_ref=coarse.at[chunk, :, origin], dst_ref=coarse.at[chunk, :, origin],
-                        send_sem=coarse_send.at[chunk, step], recv_sem=coarse_recv.at[chunk, step],
+                        src_ref=coarse.at[pair, :, origin], dst_ref=coarse.at[pair, :, origin],
+                        send_sem=coarse_send.at[pair, step], recv_sem=coarse_recv.at[pair, step],
                         device_id={"seq": partner}, device_id_type=MESH,
                     ).wait_recv()
 
@@ -441,7 +448,7 @@
                     rows_at(far, chunk, side, block, 6, QUARTER),
                     rows_at(far, chunk, side, block + 13, 6, QUARTER),
                     *near[side],
-                    coarse[chunk, side],
+                    coarse[pair, side],
                 ],
                 axis=0,
             )
@@ -451,7 +458,7 @@
             return lax.dot_general(
                 q_rows[chunk, here], atom_rows(block, 0),
                 (((1,), (1,)), ((), ())), preferred_element_type=jnp.float32,
-            ) * scale + bias[pl.ds(block, 1), :]
+            ) * scale + bias[pl.ds(chunk % 2 * GROUP_BLOCKS + block, 1), :]
 
         def finish_block(block, scores):
             here = pl.ds(pl.multiple_of(block * BLOCK, BLOCK), BLOCK)
@@ -516,11 +523,13 @@
             def _():
                 routed(route, chunk).wait_send()
 
+    @pl.loop(0, chunks // 2)
+    def _(pair):
         @pl.loop(1, groups)
         def _(step):
             @pl.when(jnp.abs(lax.rem(group + step, groups) - group) > 2)
             def _():
-                coarse_copy(chunk, step).wait_send()
+                coarse_copy(pair, step).wait_send()
 
     @pl.loop(0, chunks)
     def _(chunk):
@@ -547,14 +556,14 @@
             pltpu.VMEM((chunks, 2, FINE_BLOCKS * BLOCK, HEAD_DIM), bf16),
             pltpu.VMEM((chunks, 2, MID_BLOCKS * HALF, HEAD_DIM), bf16),
             pltpu.VMEM((chunks, 2, FAR_BLOCKS * QUARTER, HEAD_DIM), bf16),
-            pltpu.VMEM((chunks, 2, groups * COARSE_SLOT, HEAD_DIM), bf16),
+            pltpu.VMEM((chunks // 2, 2, groups * COARSE_SLOT, HEAD_DIM), bf16),
             pltpu.VMEM((chunks, 2 * rows_dev, HEAD_DIM), bf16),
-            pltpu.VMEM((8, atoms), jnp.float32),
+            pltpu.VMEM((2 * GROUP_BLOCKS, atoms), jnp.float32),
             pltpu.VMEM((STAGES, rows_dev, HEAD_DIM), jnp.float32),
             pltpu.SemaphoreType.DMA((chunks, KINDS)),
             pltpu.SemaphoreType.DMA((chunks, KINDS)),
-            pltpu.SemaphoreType.DMA((chunks, groups)),
-            pltpu.SemaphoreType.DMA((chunks, groups)),
+            pltpu.SemaphoreType.DMA((chunks // 2, groups)),
+            pltpu.SemaphoreType.DMA((chunks // 2, groups)),
             pltpu.SemaphoreType.DMA((chunks, 4)),
             pltpu.SemaphoreType.REGULAR((2,)),
         ],

time: 57.8 us -> 56.7 us (0.981)
  Pallas kernels: 56.7 us -> 55.5 us
    pallas_call x1, Pallas kernels: 56.7 us -> 55.5 us  [per_device(): pl.pallas_call(functools.partial(kernel, groups), out_shape=jax.ShapeDtyp...]
where the time goes in v3:
time: 56.7 us; the launch traced here: 56.5 us
  Pallas kernels  55.5 us (98%)
  local copies, waits for them, and re-layouts  0.97 us (2%)
    pallas_call x1, Pallas kernels, per_device(): pl.pallas_call(functools.partial(kernel, groups), out_shape=jax.ShapeDtyp...  55.5 us

profile of v3, /device:TPU:0, one launch (start us, length us, event | category | flops | bytes accessed | tf_op | source)
XLA Modules:
  0.0 56.5 jit_solution(15970886737244958966)
XLA Ops:
  0.0 55.5 %shard_map.37 = bf16[256,2048]{1,0:T(8,128)(2,1)S(1)} custom-call(bf16[256,2048]{1,0:T(8,128)(2,1)} %q_ref.1, bf16[256,2048]{1,0:T(8,128)(2,1)} %k_ref.1, bf16[256,2048]{1,0:T(8,128)(2,1)} %v_ref.1), custom_call_target="tpu_custom_call" | custom-call | tf_op jit(solution)/shard_map/pallas_call | solution.py:549
  55.5 1.0 %copy.5 = bf16[256,2048]{1,0:T(8,128)(2,1)} copy(bf16[256,2048]{1,0:T(8,128)(2,1)S(1)} %shard_map.37) | data formatting | bytes 2097152

commit v4 on v3

--- a/solution.py
+++ b/solution.py
@@ -25,7 +25,7 @@
 MID_LOW, MID_BLOCKS = -MID_REACH, GROUP_BLOCKS + 2 * MID_REACH
 FAR_LOW, FAR_BLOCKS = -FAR_REACH, GROUP_BLOCKS + 2 * FAR_REACH
 
-KIND_K, KIND_V, KIND_Q, KIND_O, KIND_EDGE_K, KIND_EDGE_V, KIND_FINE, KIND_MID_OWN = range(8)
+KIND_K, KIND_V, KIND_Q, KIND_BACK, KIND_EDGE_K, KIND_EDGE_V, KIND_FINE, KIND_MID_OWN = range(8)
 KIND_MID_OTHER, KIND_FAR = KIND_MID_OWN + 2, KIND_MID_OWN + 4
 SECOND_HOP = (
     (13, 2, -4, 4, -8, 1),
@@ -33,13 +33,14 @@
 )
 DIRECT = (
     (15, 3, 3, 1, -9, 3),
-    (16, -3, 0, 1, 12, -3),
+    (KIND_BACK, -3, 0, 1, 12, -3),
 )
 RELAY_LAG, ATTEND_LAG = 2, 4
-AHEAD, QUERY_LAG = 5, 1
+AHEAD, QUERY_LAG = 4, 2
 STAGES = 4
-KINDS = 18
-KIND_LAST = 17
+RECV_KINDS, KINDS = 16, 18
+KIND_O, KIND_LAST = 16, 17
+ALL = slice(None)
 MESH = pl.DeviceIdType.MESH
 
 
@@ -57,7 +58,7 @@
 def kernel(
     groups, q_ref, k_ref, v_ref, o_ref,
     q_rows, fine, mid, far, coarse, out_rows, bias,
-    stage, send, recv, coarse_send, coarse_recv, local, entered,
+    stage, send, recv, result_recv, coarse_send, coarse_recv, local, entered,
 ):
     me = lax.axis_index("seq")
     group = me // 2
@@ -72,17 +73,25 @@
     half_blocks = GROUP_BLOCKS // 2
 
     def own_cols(chunk):
+        if chunk is ALL:
+            return pl.ds(pl.multiple_of(parity * half_cols, HEAD_DIM), half_cols)
         return pl.ds(pl.multiple_of(parity * half_cols + chunk * HEAD_DIM, HEAD_DIM), HEAD_DIM)
 
     def other_cols(chunk):
+        if chunk is ALL:
+            return pl.ds(pl.multiple_of((1 - parity) * half_cols, HEAD_DIM), half_cols)
         return pl.ds(pl.multiple_of((1 - parity) * half_cols + chunk * HEAD_DIM, HEAD_DIM), HEAD_DIM)
 
     def fine_rows(block):
         return pl.ds(pl.multiple_of((block - FINE_LOW) * BLOCK, BLOCK), BLOCK)
 
     def remote(src, dst, kind, chunk, target):
+        if kind in (KIND_O, KIND_LAST):
+            arrived = result_recv.at[kind - KIND_O]
+        else:
+            arrived = recv.at[0 if chunk is ALL else chunk, kind]
         return pltpu.make_async_remote_copy(
-            src_ref=src, dst_ref=dst, send_sem=send.at[chunk, kind], recv_sem=recv.at[chunk, kind],
+            src_ref=src, dst_ref=dst, send_sem=send.at[kind], recv_sem=arrived,
             device_id={"seq": target}, device_id_type=MESH,
         )
 
@@ -183,13 +192,8 @@
 
     def own_result(chunk):
         return pltpu.make_async_copy(
-            out_rows.at[chunk, pl.ds(own_first, rows_dev)], o_ref.at[:, own_cols(chunk)],
-            local.at[chunk, KIND_O],
-        )
-
-    @pl.loop(0, coarse.shape[0])
-    def _(pair):
-        coarse[pair] = jnp.zeros(coarse.shape[1:], jnp.bfloat16)
+            out_rows.at[chunk, pl.ds(own_first, rows_dev)], o_ref.at[:, own_cols(chunk)], local.at[0, 3],
+        )
 
     def start_edge(chunk):
         @pl.when(inside(outward))
@@ -203,6 +207,10 @@
         @pl.when(inside(way))
         def _():
             pl.semaphore_signal(barrier, inc=1, device_id={"seq": me + 2 * way}, device_id_type=MESH)
+
+    @pl.loop(0, coarse.shape[0])
+    def _(pair):
+        coarse[pair] = jnp.zeros(coarse.shape[1:], jnp.bfloat16)
 
     pl.semaphore_wait(barrier, 1 + inside(1).astype(jnp.int32) + inside(-1).astype(jnp.int32))
 
@@ -473,11 +481,11 @@
         theirs = [(1 - parity) * half_blocks + step for step in range(half_blocks)]
         ours = [parity * half_blocks + step for step in range(half_blocks)]
         order = theirs + ours
-        scores = score_block(order[0])
+        scores = [score_block(order[0]), score_block(order[1])]
         for step in range(GROUP_BLOCKS):
-            later = score_block(order[step + 1]) if step + 1 < GROUP_BLOCKS else None
-            finish_block(order[step], scores)
-            scores = later
+            if step + 2 < GROUP_BLOCKS:
+                scores.append(score_block(order[step + 2]))
+            finish_block(order[step], scores[step])
             if step < half_blocks:
                 result_copy(step, chunk).start()
         own_result(chunk).start()
@@ -488,7 +496,7 @@
             start_edge(chunk + AHEAD)
             prepare(chunk + AHEAD)
 
-    stages = ((look_ahead, 0), (gather, 0), (relay, RELAY_LAG), (attend, ATTEND_LAG))
+    stages = ((gather, 0), (look_ahead, 0), (relay, RELAY_LAG), (attend, ATTEND_LAG))
 
     @pl.loop(0, chunks + ATTEND_LAG)
     def _(step):
@@ -497,31 +505,29 @@
             def _():
                 stage(step - lag)
 
-    @pl.loop(0, chunks)
-    def _(chunk):
-        for kind in (KIND_K, KIND_V, KIND_Q):
-            exchange(kind, chunk).wait_send()
-
-        @pl.when(inside(outward))
-        def _():
-            edge_copy(0, chunk).wait_send()
-            edge_copy(1, chunk).wait_send()
-
-        @pl.when(inside(-outward))
-        def _():
-            fine_copy(chunk).wait_send()
-
-        for way in (-1, 1):
-            @pl.when(inside(way))
-            def _():
-                mid_copy(0, way, chunk).wait_send()
-                mid_copy(1, way, chunk).wait_send()
-                far_copy(way, chunk).wait_send()
-
-        for route in SECOND_HOP + DIRECT:
-            @pl.when(inside(route[5]) & inside(route[5] - route[1]))
-            def _():
-                routed(route, chunk).wait_send()
+    for kind in (KIND_K, KIND_V, KIND_Q):
+        exchange(kind, ALL).wait_send()
+
+    @pl.when(inside(outward))
+    def _():
+        edge_copy(0, ALL).wait_send()
+        edge_copy(1, ALL).wait_send()
+
+    @pl.when(inside(-outward))
+    def _():
+        fine_copy(ALL).wait_send()
+
+    for way in (-1, 1):
+        @pl.when(inside(way))
+        def _():
+            mid_copy(0, way, ALL).wait_send()
+            mid_copy(1, way, ALL).wait_send()
+            far_copy(way, ALL).wait_send()
+
+    for route in SECOND_HOP + DIRECT:
+        @pl.when(inside(route[5]) & inside(route[5] - route[1]))
+        def _():
+            routed(route, ALL).wait_send()
 
     @pl.loop(0, chunks // 2)
     def _(pair):
@@ -531,12 +537,11 @@
             def _():
                 coarse_copy(pair, step).wait_send()
 
-    @pl.loop(0, chunks)
-    def _(chunk):
-        own_result(chunk).wait()
-        for step in range(half_blocks):
-            result_copy(step, chunk).wait_send()
-            result_copy(step, chunk).wait_recv()
+    whole = q_rows.at[:, pl.ds(own_first, rows_dev)]
+    pltpu.make_async_copy(whole, whole, local.at[0, 3]).wait()
+    for step in range(half_blocks):
+        result_copy(step, ALL).wait_send()
+        result_copy(step, ALL).wait_recv()
 
 
 def per_device(queries, key_rows, value_rows):
@@ -560,8 +565,9 @@
             pltpu.VMEM((chunks, 2 * rows_dev, HEAD_DIM), bf16),
             pltpu.VMEM((2 * GROUP_BLOCKS, atoms), jnp.float32),
             pltpu.VMEM((STAGES, rows_dev, HEAD_DIM), jnp.float32),
-            pltpu.SemaphoreType.DMA((chunks, KINDS)),
-            pltpu.SemaphoreType.DMA((chunks, KINDS)),
+            pltpu.SemaphoreType.DMA((KINDS,)),
+            pltpu.SemaphoreType.DMA((chunks, RECV_KINDS)),
+            pltpu.SemaphoreType.DMA((2,)),
             pltpu.SemaphoreType.DMA((chunks // 2, groups)),
             pltpu.SemaphoreType.DMA((chunks // 2, groups)),
             pltpu.SemaphoreType.DMA((chunks, 4)),

time: 56.7 us -> 55.1 us (0.972)
  Pallas kernels: 55.5 us -> 54 us
    pallas_call x1, Pallas kernels: 55.5 us -> 54 us  [per_device(): pl.pallas_call(functools.partial(kernel, groups), out_shape=jax.ShapeDtyp...]
where the time goes in v4:
time: 55.1 us; the launch traced here: 55 us
  Pallas kernels  54 us (98%)
  local copies, waits for them, and re-layouts  0.97 us (2%)
    pallas_call x1, Pallas kernels, per_device(): pl.pallas_call(functools.partial(kernel, groups), out_shape=jax.ShapeDtyp...  54 us

profile of v4, /device:TPU:0, one launch (start us, length us, event | category | flops | bytes accessed | tf_op | source)
XLA Modules:
  0.0 55.0 jit_solution(3523207851224417230)
XLA Ops:
  0.0 54.0 %shard_map.37 = bf16[256,2048]{1,0:T(8,128)(2,1)S(1)} custom-call(bf16[256,2048]{1,0:T(8,128)(2,1)} %q_ref.1, bf16[256,2048]{1,0:T(8,128)(2,1)} %k_ref.1, bf16[256,2048]{1,0:T(8,128)(2,1)} %v_ref.1), custom_call_target="tpu_custom_call" | custom-call | tf_op jit(solution)/shard_map/pallas_call | solution.py:554
  54.0 1.0 %copy.5 = bf16[256,2048]{1,0:T(8,128)(2,1)} copy(bf16[256,2048]{1,0:T(8,128)(2,1)S(1)} %shard_map.37) | data formatting | bytes 2097152

commit v5 on v4

--- a/solution.py
+++ b/solution.py
@@ -38,7 +38,8 @@
 RELAY_LAG, ATTEND_LAG = 2, 4
 AHEAD, QUERY_LAG = 4, 2
 STAGES = 4
-RECV_KINDS, KINDS = 16, 18
+RECV_OF = (0, 0, 1, 2, 3, 3, 4, 5, 6, 5, 6, 5, 6, 7, 8, 9)
+RECV_KINDS, KINDS = 10, 18
 KIND_O, KIND_LAST = 16, 17
 ALL = slice(None)
 MESH = pl.DeviceIdType.MESH
@@ -89,7 +90,7 @@
         if kind in (KIND_O, KIND_LAST):
             arrived = result_recv.at[kind - KIND_O]
         else:
-            arrived = recv.at[0 if chunk is ALL else chunk, kind]
+            arrived = recv.at[0 if chunk is ALL else chunk, RECV_OF[kind]]
         return pltpu.make_async_remote_copy(
             src_ref=src, dst_ref=dst, send_sem=send.at[kind], recv_sem=arrived,
             device_id={"seq": target}, device_id_type=MESH,
@@ -167,6 +168,9 @@
             device_id={"seq": target}, device_id_type=MESH,
         )
 
+    def await_bytes(ref, semaphore):
+        pltpu.make_async_copy(ref, ref, semaphore).wait()
+
     def inside(offset):
         return (group + offset >= 0) & (group + offset < groups)
 
@@ -188,11 +192,11 @@
         else:
             source = k_ref if kind == KIND_K else v_ref
             target = fine.at[chunk, kind, pl.ds(BLOCK + own_first, rows_dev)]
-        return pltpu.make_async_copy(source.at[:, own_cols(chunk)], target, local.at[chunk, kind])
+        return pltpu.make_async_copy(source.at[:, own_cols(chunk)], target, local.at[chunk, kind // 2])
 
     def own_result(chunk):
         return pltpu.make_async_copy(
-            out_rows.at[chunk, pl.ds(own_first, rows_dev)], o_ref.at[:, own_cols(chunk)], local.at[0, 3],
+            out_rows.at[chunk, pl.ds(own_first, rows_dev)], o_ref.at[:, own_cols(chunk)], result_recv.at[2],
         )
 
     def start_edge(chunk):
@@ -261,8 +265,7 @@
             far[chunk, side, pl.ds(pl.multiple_of(-FAR_LOW * QUARTER + first // 4, QUARTER), rows_dev // 4)] = fours
 
     def prepare(chunk):
-        own_copy(KIND_K, chunk).wait()
-        own_copy(KIND_V, chunk).wait()
+        await_bytes(fine.at[chunk, :, pl.ds(BLOCK + own_first, rows_dev)], local.at[chunk, 0])
         pool_half(chunk, parity)
         for way in (-1, 1):
             @pl.when(inside(way))
@@ -354,8 +357,7 @@
         return pooled(far[chunk, side, first : first + GROUP_ROWS // 4], COARSE_SLOT, POOL // 4)
 
     def gather(chunk):
-        for kind in (KIND_K, KIND_V):
-            exchange(kind, chunk).wait_recv()
+        await_bytes(fine.at[chunk, :, pl.ds(BLOCK + other_first, rows_dev)], recv.at[chunk, RECV_OF[KIND_K]])
 
         @pl.when(inside(-outward))
         def _():
@@ -391,8 +393,7 @@
     def relay(chunk):
         @pl.when(inside(-outward))
         def _():
-            edge_copy(0, chunk).wait_recv()
-            edge_copy(1, chunk).wait_recv()
+            await_bytes(fine.at[chunk, :, :BLOCK], recv.at[chunk, RECV_OF[KIND_EDGE_K]])
 
         @pl.when(inside(outward))
         def _():
@@ -401,9 +402,9 @@
         for way in (-1, 1):
             @pl.when(inside(-way))
             def _():
-                mid_copy(0, way, chunk).wait_recv()
-                mid_copy(1, way, chunk).wait_recv()
-                far_copy(way, chunk).wait_recv()
+                await_bytes(
+                    far.at[chunk, :, : 2 * HALF + QUARTER], recv.at[chunk, RECV_OF[KIND_FAR + (way < 0)]]
+                )
 
         for side in range(2):
             for end, near_mid in ((0, 0), (GROUP_BLOCKS + 1, GROUP_BLOCKS + MID_REACH + 1)):
@@ -538,7 +539,7 @@
                 coarse_copy(pair, step).wait_send()
 
     whole = q_rows.at[:, pl.ds(own_first, rows_dev)]
-    pltpu.make_async_copy(whole, whole, local.at[0, 3]).wait()
+    await_bytes(whole, result_recv.at[2])
     for step in range(half_blocks):
         result_copy(step, ALL).wait_send()
         result_copy(step, ALL).wait_recv()
@@ -567,10 +568,10 @@
             pltpu.VMEM((STAGES, rows_dev, HEAD_DIM), jnp.float32),
             pltpu.SemaphoreType.DMA((KINDS,)),
             pltpu.SemaphoreType.DMA((chunks, RECV_KINDS)),
-            pltpu.SemaphoreType.DMA((2,)),
+            pltpu.SemaphoreType.DMA((3,)),
             pltpu.SemaphoreType.DMA((chunks // 2, groups)),
             pltpu.SemaphoreType.DMA((chunks // 2, groups)),
-            pltpu.SemaphoreType.DMA((chunks, 4)),
+            pltpu.SemaphoreType.DMA((chunks, 2)),
             pltpu.SemaphoreType.REGULAR((2,)),
         ],
         compiler_params=pltpu.CompilerParams(

time: 55.1 us -> 54.5 us (0.989)
  Pallas kernels: 54 us -> 53.4 us
    pallas_call x1, Pallas kernels: 54 us -> 53.4 us  [per_device(): pl.pallas_call(functools.partial(kernel, groups), out_shape=jax.ShapeDtyp...]
where the time goes in v5:
time: 54.5 us; the launch traced here: 54.4 us
  Pallas kernels  53.4 us (98%)
  local copies, waits for them, and re-layouts  0.97 us (2%)
    pallas_call x1, Pallas kernels, per_device(): pl.pallas_call(functools.partial(kernel, groups), out_shape=jax.ShapeDtyp...  53.4 us

profile of v5, /device:TPU:0, one launch (start us, length us, event | category | flops | bytes accessed | tf_op | source)
XLA Modules:
  0.0 54.4 jit_solution(6751095043778918167)
XLA Ops:
  0.0 53.4 %shard_map.37 = bf16[256,2048]{1,0:T(8,128)(2,1)S(1)} custom-call(bf16[256,2048]{1,0:T(8,128)(2,1)} %q_ref.1, bf16[256,2048]{1,0:T(8,128)(2,1)} %k_ref.1, bf16[256,2048]{1,0:T(8,128)(2,1)} %v_ref.1), custom_call_target="tpu_custom_call" | custom-call | tf_op jit(solution)/shard_map/pallas_call | solution.py:555
  53.4 1.0 %copy.5 = bf16[256,2048]{1,0:T(8,128)(2,1)} copy(bf16[256,2048]{1,0:T(8,128)(2,1)S(1)} %shard_map.37) | data formatting | bytes 2097152

commit v6 on v5

--- a/solution.py
+++ b/solution.py
@@ -164,7 +164,7 @@
         slot = pl.ds(pl.multiple_of(group * COARSE_SLOT, COARSE_SLOT), COARSE_SLOT)
         return pltpu.make_async_remote_copy(
             src_ref=coarse.at[pair, :, slot], dst_ref=coarse.at[pair, :, slot],
-            send_sem=coarse_send.at[pair, step], recv_sem=coarse_recv.at[pair, step],
+            send_sem=coarse_send.at[step], recv_sem=coarse_recv.at[pair, step],
             device_id={"seq": target}, device_id_type=MESH,
         )
 
@@ -442,7 +442,7 @@
                 def _():
                     pltpu.make_async_remote_copy(
                         src_ref=coarse.at[pair, :, origin], dst_ref=coarse.at[pair, :, origin],
-                        send_sem=coarse_send.at[pair, step], recv_sem=coarse_recv.at[pair, step],
+                        send_sem=coarse_send.at[step], recv_sem=coarse_recv.at[pair, step],
                         device_id={"seq": partner}, device_id_type=MESH,
                     ).wait_recv()
 
@@ -530,13 +530,15 @@
         def _():
             routed(route, ALL).wait_send()
 
-    @pl.loop(0, chunks // 2)
-    def _(pair):
-        @pl.loop(1, groups)
-        def _(step):
-            @pl.when(jnp.abs(lax.rem(group + step, groups) - group) > 2)
-            def _():
-                coarse_copy(pair, step).wait_send()
+    @pl.loop(1, groups)
+    def _(step):
+        @pl.when(jnp.abs(lax.rem(group + step, groups) - group) > 2)
+        def _():
+            pltpu.make_async_remote_copy(
+                src_ref=coarse.at[:, :, :COARSE_SLOT], dst_ref=coarse.at[:, :, :COARSE_SLOT],
+                send_sem=coarse_send.at[step], recv_sem=coarse_recv.at[0, step],
+                device_id={"seq": partner}, device_id_type=MESH,
+            ).wait_send()
 
     whole = q_rows.at[:, pl.ds(own_first, rows_dev)]
     await_bytes(whole, result_recv.at[2])
@@ -569,7 +571,7 @@
             pltpu.SemaphoreType.DMA((KINDS,)),
             pltpu.SemaphoreType.DMA((chunks, RECV_KINDS)),
             pltpu.SemaphoreType.DMA((3,)),
-            pltpu.SemaphoreType.DMA((chunks // 2, groups)),
+            pltpu.SemaphoreType.DMA((groups,)),
             pltpu.SemaphoreType.DMA((chunks // 2, groups)),
             pltpu.SemaphoreType.DMA((chunks, 2)),
             pltpu.SemaphoreType.REGULAR((2,)),

time: 54.5 us -> 54.4 us (level)
  no operation moved by 1% of the time
where the time goes in v6:
time: 54.4 us; the launch traced here: 54.3 us
  Pallas kernels  53.3 us (98%)
  local copies, waits for them, and re-layouts  0.97 us (2%)
    pallas_call x1, Pallas kernels, per_device(): pl.pallas_call(functools.partial(kernel, groups), out_shape=jax.ShapeDtyp...  53.3 us

profile of v6, /device:TPU:0, one launch (start us, length us, event | category | flops | bytes accessed | tf_op | source)
XLA Modules:
  0.0 54.3 jit_solution(3598526109424725486)
XLA Ops:
  0.0 53.3 %shard_map.37 = bf16[256,2048]{1,0:T(8,128)(2,1)S(1)} custom-call(bf16[256,2048]{1,0:T(8,128)(2,1)} %q_ref.1, bf16[256,2048]{1,0:T(8,128)(2,1)} %k_ref.1, bf16[256,2048]{1,0:T(8,128)(2,1)} %v_ref.1), custom_call_target="tpu_custom_call" | custom-call | tf_op jit(solution)/shard_map/pallas_call | solution.py:557
  53.3 1.0 %copy.5 = bf16[256,2048]{1,0:T(8,128)(2,1)} copy(bf16[256,2048]{1,0:T(8,128)(2,1)S(1)} %shard_map.37) | data formatting | bytes 2097152
